TPU v7x, 512 devices: a whole 4x8x8 slice. The times are simulated.
512 devices in a mesh: seq: 128 (over x, z, y_lo), head: 4 (over y_hi, core).
Axes of the slice: x: 4, y: 8 (y_hi: 2, y_lo: 4; y = y_hi * 4 + y_lo), z: 8, core: 2. Of those that a mesh axis runs over, the one named last changes fastest.
Arguments:
- features: bfloat16 [32768, 1024], P('seq', 'head'), may hold values from -6 to 6
- w_query: bfloat16 [1024, 512], P(None, 'head'), may hold values from -0.1875 to 0.1875
- w_key: bfloat16 [1024, 512], P(None, 'head'), may hold values from -0.1875 to 0.1875
- w_value: bfloat16 [1024, 1024], P(None, 'head'), may hold values from -0.1875 to 0.1875
- w_gate: bfloat16 [1024, 1024], P(None, 'head'), may hold values from -0.1875 to 0.1875
- w_out: bfloat16 [1024, 1024], replicated, may hold values from -0.1875 to 0.1875
- forget: bfloat16 [2, 32768, 512], P(None, 'seq', 'head'), may hold values from -2.5 to 0, as said below
Outputs:
- encoded: bfloat16 [32768, 1024], P('seq', 'head')
Inputs may be any that keep to these rules, and one draw needn't show every extreme that they name: `forget`: every entry is below zero.
All inputs are finite; a program needn't handle non-finite values.
Results may differ from a plain program's by a relative error of at most 0.013.
Values may be sent and summed in bfloat16 or wider, within the bound.
A program may use at most 64 MiB of HBM per device.

v0:
```python
import jax
import jax.numpy as jnp
from jax import lax
from jax.sharding import Mesh
from jax.sharding import PartitionSpec as P

HEAD_K = 64
HEAD_V = 128
GROUP = 64
SEQ = ("seq_0", "seq_1", "seq_2")


def from_everyone(shard, axis):
    copies = jnp.broadcast_to(shard, (lax.axis_size(axis), *shard.shape))
    return lax.all_to_all(copies, axis, split_axis=0, concat_axis=0, tiled=True)


def in_order(tiles, dim):
    dims = list(tiles.shape[1:])
    dims[dim] *= tiles.shape[0]
    return jnp.moveaxis(tiles, 0, dim).reshape(dims)


def collect(shard, axis, dim):
    tiles = from_everyone(shard, axis)
    return in_order(tiles, dim)


def nothing_yet(shard, identity):
    return jax.tree.map(
        lambda a, e: jnp.broadcast_to(jnp.asarray(e, a.dtype), a.shape), shard, identity
    )


def gathered_once(shard, axis):
    leaves = jax.tree.leaves(shard)
    order = sorted(range(len(leaves)), key=lambda k: -leaves[k].size)
    width = (1, *leaves[order[0]].shape)[-1]
    lines = [
        jnp.pad(leaves[k].reshape(-1), (0, -leaves[k].size % width)).reshape(-1, width)
        for k in order
    ]
    both, at, found = (lax.all_gather(jnp.concatenate(lines), axis), 0, {})
    for k, line in zip(order, lines):
        slab = both[:, at : at + len(line)].reshape(len(both), -1)
        found[k] = slab[:, : leaves[k].size].reshape(-1, *leaves[k].shape)
        at += len(line)
    numbers = iter(range(len(leaves)))
    return jax.tree.map(lambda _: found[next(numbers)], shard)


def prefix_by_axis(shard, axes, combine, identity):
    before = start = nothing_yet(shard, identity)
    so_far = shard
    for axis in reversed(axes):
        peers, place = (lax.axis_size(axis), lax.axis_index(axis))
        pieces = gathered_once(so_far, axis)
        inside, so_far = (start, start)
        for k in range(peers):
            passed = k < place
            so_far = combine(so_far, jax.tree.map(lambda part: part[k], pieces))
            inside = jax.tree.map(lambda new, old: jnp.where(passed, new, old), so_far, inside)
        before = combine(inside, before)
    return before


def carried_in(shard, axes, combine, identity):
    before = start = nothing_yet(shard, identity)
    so_far = shard
    for axis in reversed(axes):
        peers, place = (lax.axis_size(axis), lax.axis_index(axis))
        pieces = gathered_once(
            jax.tree.map(
                lambda part, kind: part.astype(kind), so_far, (jnp.bfloat16, jnp.bfloat16)
            ),
            axis,
        )
        inside, so_far = (start, start)
        for k in reversed(range(peers)):
            passed = k > place
            so_far = combine(
                so_far, jax.tree.map(lambda part, own: part[k].astype(own.dtype), pieces, shard)
            )
            inside = jax.tree.map(lambda new, old: jnp.where(passed, new, old), so_far, inside)
        before = combine(inside, before)
    return before


def to_blocks(tensor):
    block_count = tensor.shape[0] // GROUP
    return tensor.reshape((block_count, GROUP) + tensor.shape[1:])


def state_increment(memory, key_block, value_block, running):
    finale = running[-1]
    key_to_end = (key_block.astype(jnp.float32) * jnp.exp(finale[None] - running)).astype(
        jnp.bfloat16
    )
    added = jnp.einsum("shi,shj->hij", key_to_end, value_block, preferred_element_type=jnp.float32)
    return jnp.exp(finale)[:, :, None] * memory + added


def block_pass(query_matrix, key_rows, value_rows, decays, initial):
    triangle = jnp.tril(jnp.ones((GROUP, GROUP), jnp.float32))

    def block_advance(memory, blocks):
        query_block, key_block, value_block, decay_block = blocks
        running = jnp.cumsum(decay_block, axis=0)
        query_decayed = (query_block.astype(jnp.float32) * jnp.exp(running)).astype(jnp.bfloat16)
        key_grown = (key_block.astype(jnp.float32) * jnp.exp(-running)).astype(jnp.bfloat16)
        scores = (
            jnp.einsum("thi,shi->hts", query_decayed, key_grown, preferred_element_type=jnp.float32)
            * triangle
        )
        within = jnp.einsum(
            "hts,shj->thj",
            scores.astype(jnp.bfloat16),
            value_block,
            preferred_element_type=jnp.float32,
        )
        carried = jnp.einsum("thi,hij->thj", query_decayed.astype(jnp.float32), memory)
        memory = state_increment(memory, key_block, value_block, running)
        return (memory, within + carried)

    blocks = tuple((to_blocks(tensor) for tensor in (query_matrix, key_rows, value_rows, decays)))
    last_memory, outputs = lax.scan(block_advance, initial, blocks)
    return outputs.reshape((query_matrix.shape[0],) + outputs.shape[2:])


def device_summary(key_rows, value_rows, decays):
    heads_here = key_rows.shape[1]

    def device_advance(memory, blocks):
        key_block, value_block, decay_block = blocks
        running = jnp.cumsum(decay_block, axis=0)
        return (state_increment(memory, key_block, value_block, running), None)

    initial = jnp.zeros((heads_here, HEAD_K, HEAD_V), jnp.float32)
    memory, unused = lax.scan(
        device_advance,
        initial,
        tuple((to_blocks(tensor) for tensor in (key_rows, value_rows, decays))),
    )
    total = jnp.sum(decays, axis=0)
    return (total.reshape(-1), memory.reshape(-1, memory.shape[2]))


def combine_states(earlier, latter):
    return (earlier[0] + latter[0], jnp.exp(latter[0])[:, None] * earlier[1] + latter[1])


def local(features, w_query, w_key, w_value, w_gate, w_out, forget):
    row_count = features.shape[0]
    heads_here = w_query.shape[1] // HEAD_K
    columns = collect(features, "head", 1)
    query_sum, key_sum, value_sum, gating = tuple(
        (
            jnp.dot(columns, weight, preferred_element_type=jnp.float32)
            for weight in (w_query, w_key, w_value, w_gate)
        )
    )
    query_matrix = (query_sum * 0.125).astype(jnp.bfloat16).reshape(row_count, heads_here, HEAD_K)
    key_rows = key_sum.astype(jnp.bfloat16).reshape(row_count, heads_here, HEAD_K)
    value_rows = value_sum.astype(jnp.bfloat16).reshape(row_count, heads_here, HEAD_V)
    decays = forget.astype(jnp.float32).reshape(2, row_count, heads_here, HEAD_K)
    flipped_queries = jnp.flip(query_matrix, 0)
    flipped_keys = jnp.flip(key_rows, 0)
    flipped_values = jnp.flip(value_rows, 0)
    flipped_decays = jnp.flip(decays[1], 0)
    ahead_total, ahead_memory = device_summary(key_rows, value_rows, decays[0])
    behind_total, behind_memory = device_summary(flipped_keys, flipped_values, flipped_decays)
    identity = (jnp.zeros_like(ahead_total), jnp.zeros_like(ahead_memory))
    ahead_inflow = prefix_by_axis((ahead_total, ahead_memory), SEQ, combine_states, identity)[1]
    behind_inflow = carried_in((behind_total, behind_memory), SEQ, combine_states, identity)[1]
    ahead_out = block_pass(
        query_matrix,
        key_rows,
        value_rows,
        decays[0],
        ahead_inflow.reshape(heads_here, HEAD_K, HEAD_V),
    )
    behind_flipped = block_pass(
        flipped_queries,
        flipped_keys,
        flipped_values,
        flipped_decays,
        behind_inflow.reshape(heads_here, HEAD_K, HEAD_V),
    )
    mixture = ahead_out + jnp.flip(behind_flipped, 0)
    scaled = mixture * lax.rsqrt(jnp.mean(mixture * mixture, axis=-1, keepdims=True) + 1e-06)
    normed = (scaled.reshape(row_count, heads_here * HEAD_V) * jax.nn.silu(gating)).astype(
        jnp.bfloat16
    )
    out_width = w_out.shape[1] // lax.axis_size("head")
    own_columns = lax.dynamic_slice_in_dim(w_out, lax.axis_index("head") * out_width, out_width, 1)
    encoded = jnp.dot(
        lax.all_gather(normed, "head", axis=1, tiled=True),
        own_columns,
        preferred_element_type=jnp.float32,
    )
    return encoded.astype(jnp.bfloat16)


def solution(mesh):
    torus = Mesh(
        mesh.devices.reshape(4, 8, 4, mesh.shape["head"]), ("seq_0", "seq_1", "seq_2", "head")
    )
    placed = (
        P(SEQ, "head"),
        P(None, "head"),
        P(None, "head"),
        P(None, "head"),
        P(None, "head"),
        P(),
        P(None, SEQ, "head"),
    )
    return jax.shard_map(
        local, mesh=torus, in_specs=placed, out_specs=P(SEQ, "head"), check_vma=False
    )
```

profile of v0, /device:TPU:1, one launch (start us, length us, event | category | flops | bytes accessed | tf_op | source)
XLA Modules:
  0.0 234.6 jit_solution(15789298678491646530)
XLA Ops:
  2.0 10.3 %all-to-all-start = ((bf16[4,256,256]{1,2,0:T(8,128)(2,1)}), bf16[4,256,256]{1,2,0:T(8,128)(2,1)S(1)}, u32[]{:S(2)}, u32[]{:S(2)}) async-start(bf16[4,256,256]{1,2,0:T(8,128)(2,1)} %broadcast_in_dim.16), calls=%async_computation | async-start | bytes 1048576 | tf_op jit(solution)/shard_map/all_to_all | solution.py:15
  15.0 11.3 %all-to-all-done = bf16[4,256,256]{1,2,0:T(8,128)(2,1)S(1)} async-done(((bf16[4,256,256]{1,2,0:T(8,128)(2,1)}), bf16[4,256,256]{1,2,0:T(8,128)(2,1)S(1)}, u32[]{:S(2)}, u32[]{:S(2)}) %all-to-all-start) | async-done | bytes 524320 | tf_op jit(solution)/shard_map/all_to_all | solution.py:15
  31.3 2.8 %rev.21 = bf16[256,2,128]{2,0,1:T(8,128)(2,1)} reverse(bf16[256,2,128]{2,0,1:T(8,128)(2,1)} %copy.69), dimensions={0} | reverse | bytes 262144 | tf_op jit(solution)/shard_map/jit(_flip)/rev | solution.py:168
  36.0 4.5 %while.51 = (s32[]{:T(128)}, f32[2,64,128]{2,1,0:T(8,128)S(1)}, f32[4,64,2,64]{3,2,1,0:T(2,128)S(1)}, bf16[4,64,2,64]{3,2,1,0:T(2,128)(2,1)}, bf16[4,64,2,128]{3,1,2,0:T(8,128)(2,1)S(1)}, /*index=5*/s32[]{:T(128)}, s32[]{:T(128)}) while((s32[]{:T(128)}, f32[2,64,128]{2,1,0:T(8,128)S(1)}, f32[4,64,2,64]{3,2,1,0:T(2,128)S(1)}, ...), condition=%wide.region_9.10_spmd.clone, body=%wide.region_7.9_spmd.clone.sunk | while | flops 2695171 | bytes 364131 | solution.py:139
  40.6 11.2 %all-gather.9 = bf16[4,129,128]{2,1,0:T(8,128)(2,1)S(1)} all-gather(bf16[1,129,128]{2,1,0:T(8,128)(2,1)S(1)} %maximum_bitcast_fusion.3), channel_id=5, replica_groups=mesh['seq_0'=4,'seq_1'=8,'seq_2'=4,'head'=4] {'seq_2'}, dimensions={0}, use_global_device_ids=true | all-gather | bytes 165120 | tf_op jit(solution)/shard_map/all_gather | solution.py:43
  53.1 25.6 %all-gather.10 = bf16[8,129,128]{2,1,0:T(8,128)(2,1)S(1)} all-gather(bf16[1,129,128]{2,1,0:T(8,128)(2,1)S(1)} %maximum_bitcast_fusion.4), channel_id=6, replica_groups=mesh['seq_0'=4,'seq_1'=8,'seq_2'=4,'head'=4] {'seq_1'}, dimensions={0}, use_global_device_ids=true | all-gather | bytes 297216 | tf_op jit(solution)/shard_map/all_gather | solution.py:43
  80.0 1.7 copy.62
  81.8 1.7 copy.61
  83.5 7.6 %while.50 = (s32[]{:T(128)}, f32[2,64,128]{2,1,0:T(8,128)S(1)}, f32[4,64,2,64]{3,2,1,0:T(2,128)S(1)}, bf16[4,64,2,64]{3,2,1,0:T(2,128)(2,1)}, bf16[4,64,2,128]{3,1,2,0:T(8,128)(2,1)}, /*index=5*/s32[]{:T(128)}, s32[]{:T(128)}) while((s32[]{:T(128)}, f32[2,64,128]{2,1,0:T(8,128)S(1)}, f32[4,64,2,64]{3,2,1,0:T(2,128)S(1)}, ...), condition=%wide.region_2.3_spmd.clone, body=%wide.region_0.2_spmd.clone.sunk | while | flops 2695171 | bytes 347743 | solution.py:139
  91.1 11.0 %all-gather.6 = f32[4,129,128]{2,1,0:T(8,128)S(1)} all-gather(f32[1,129,128]{2,1,0:T(8,128)S(1)} %maximum_bitcast_fusion), channel_id=2, replica_groups=mesh['seq_0'=4,'seq_1'=8,'seq_2'=4,'head'=4] {'seq_2'}, dimensions={0}, use_global_device_ids=true | all-gather | bytes 330240 | tf_op jit(solution)/shard_map/all_gather | solution.py:43
  102.8 1.7 slice_convert_fusion.7
  104.7 19.2 %all-gather.7 = f32[8,129,128]{2,1,0:T(8,128)S(1)} all-gather(f32[1,129,128]{2,1,0:T(8,128)S(1)} %maximum_bitcast_fusion.1), channel_id=3, replica_groups=mesh['seq_0'=4,'seq_1'=8,'seq_2'=4,'head'=4] {'seq_1'}, dimensions={0}, use_global_device_ids=true | all-gather | bytes 594432 | tf_op jit(solution)/shard_map/all_gather | solution.py:43
  125.0 10.0 %all-gather.8 = f32[4,129,128]{2,1,0:T(8,128)S(1)} all-gather(f32[1,129,128]{2,1,0:T(8,128)S(1)} %maximum_bitcast_fusion.2), channel_id=4, replica_groups=mesh['seq_0'=4,'seq_1'=8,'seq_2'=4,'head'=4] {'seq_0'}, dimensions={0}, use_global_device_ids=true | all-gather | bytes 330240 | tf_op jit(solution)/shard_map/all_gather | solution.py:43
  135.9 9.3 %all-gather.11 = bf16[4,129,128]{2,1,0:T(8,128)(2,1)S(1)} all-gather(bf16[1,129,128]{2,1,0:T(8,128)(2,1)S(1)} %maximum_bitcast_fusion.5), channel_id=7, replica_groups=mesh['seq_0'=4,'seq_1'=8,'seq_2'=4,'head'=4] {'seq_0'}, dimensions={0}, use_global_device_ids=true | all-gather | bytes 165120 | tf_op jit(solution)/shard_map/all_gather | solution.py:43
  153.2 15.1 %while.48 = (s32[]{:T(128)}, f32[2,64,128]{2,1,0:T(8,128)S(1)}, f32[4,64,2,128]{3,1,0,2:T(8,128)}, f32[4,64,2,64]{3,2,1,0:T(2,128)S(1)}, bf16[4,64,2,64]{3,2,1,0...) while((s32[]{:T(128)}, f32[2,64,128]{2,1,0:T(8,128)S(1)}, ...), condition=%wide.region_6.7_spmd.clone, body=%wide.region_4.6_spmd.clone.sunk | while | flops 8011778 | bytes 774749 | solution.py:126
  154.4 1.6 fusion.262
  158.2 1.6 fusion.262
  161.9 1.6 fusion.262
  165.7 1.6 fusion.262
  181.4 15.1 %while.49 = (s32[]{:T(128)}, f32[2,64,128]{2,1,0:T(8,128)S(1)}, f32[4,64,2,128]{3,1,0,2:T(8,128)}, f32[4,64,2,64]{3,2,1,0:T(2,128)S(1)}, bf16[4,64,2,64]{3,2,1,0...) while((s32[]{:T(128)}, f32[2,64,128]{2,1,0:T(8,128)S(1)}, ...), condition=%wide.region_13.14_spmd.clone, body=%wide.region_11.13_spmd.clone.sunk | while | flops 8011778 | bytes 774749 | solution.py:126
  186.3 1.6 fusion.275
  193.9 1.6 fusion.275
  196.5 1.7 rev.23
  200.0 33.7 %all_gather.51 = bf16[256,1024]{1,0:T(8,128)(2,1)S(1)} all-gather(bf16[256,256]{1,0:T(8,128)(2,1)S(1)} %fusion.78), channel_id=1, replica_groups=mesh['seq_0'=4,'seq_1'=8,'seq_2'=4,'head'=4] {'head'}, dimensions={1}, use_global_device_ids=true | all-gather | bytes 655360 | tf_op jit(solution)/shard_map/all_gather | solution.py:197
  (218 shorter events, 72.7 us)
Async XLA Ops:
  0.0 233.7 %copy-start = (bf16[1024,1024]{1,0:T(8,128)(2,1)S(1)}, bf16[1024,1024]{1,0:T(8,128)(2,1)}, u32[]{:S(2)}) copy-start(bf16[1024,1024]{1,0:T(8,128)(2,1)} %param.20) | copy-start | bytes 6291460
  0.0 12.3 %copy-start.5 = (bf16[2,256,128]{2,1,0:T(8,128)(2,1)S(1)}, bf16[2,256,128]{2,1,0:T(8,128)(2,1)}, u32[]{:S(2)}) copy-start(bf16[2,256,128]{2,1,0:T(8,128)(2,1)} %param.21) | copy-start | bytes 393220
  2.0 24.3 %all-to-all-start = ((bf16[4,256,256]{1,2,0:T(8,128)(2,1)}), bf16[4,256,256]{1,2,0:T(8,128)(2,1)S(1)}, u32[]{:S(2)}, u32[]{:S(2)}) async-start(bf16[4,256,256]{1,2,0:T(8,128)(2,1)} %broadcast_in_dim.16), calls=%async_computation | async-start | bytes 1048576 | tf_op jit(solution)/shard_map/all_to_all | solution.py:15
  40.6 50.6 %copy-start.1 = (bf16[4,64,2,128]{3,1,2,0:T(8,128)(2,1)}, bf16[4,64,2,128]{3,1,2,0:T(8,128)(2,1)S(1)}, u32[]{:S(2)}) copy-start(bf16[4,64,2,128]{3,1,2,0:T(8,128)(2,1)S(1)} %get-tuple-element.688) | copy-start | bytes 393220
  78.7 0.7 copy-start.2
  104.5 31.2 %copy-start.3 = (bf16[8,129,128]{2,1,0:T(8,128)(2,1)S(1)}, bf16[8,129,128]{2,1,0:T(8,128)(2,1)}, u32[]{:S(2)}) copy-start(bf16[8,129,128]{2,1,0:T(8,128)(2,1)} %copy-done.2) | copy-start | bytes 792580
  104.5 31.4 %copy-start.6 = (bf16[1,128]{1,0:T(2,128)(2,1)S(1)}, bf16[1,128]{1,0:T(2,128)(2,1)}, u32[]{:S(2)}) copy-start(bf16[1,128]{1,0:T(2,128)(2,1)} %convert_bitcast_fusion) | copy-start | bytes 772
  153.2 18.0 %copy-start.7 = (f32[1,1,128]{2,1,0:T(1,128)S(1)}, f32[1,1,128]{2,1,0:T(1,128)}, u32[]{:S(2)}) copy-start(f32[1,1,128]{2,1,0:T(1,128)} %get-tuple-element.415) | copy-start | bytes 1540
  153.2 24.7 %copy-start.10 = (f32[128]{0:T(128)S(1)}, f32[128]{0:T(128)}, u32[]{:S(2)}) copy-start(f32[128]{0:T(128)} %get-tuple-element.307) | copy-start | bytes 1540
  153.2 24.8 %copy-start.9 = (f32[128]{0:T(128)S(1)}, f32[128]{0:T(128)}, u32[]{:S(2)}) copy-start(f32[128]{0:T(128)} %get-tuple-element.308) | copy-start | bytes 1540
  153.2 24.8 %copy-start.8 = (f32[128]{0:T(128)S(1)}, f32[128]{0:T(128)}, u32[]{:S(2)}) copy-start(f32[128]{0:T(128)} %get-tuple-element.306) | copy-start | bytes 1540
  181.4 16.8 %copy-start.4 = (f32[4,64,2,128]{3,1,0,2:T(8,128)S(1)}, f32[4,64,2,128]{3,1,0,2:T(8,128)}, u32[]{:S(2)}) copy-start(f32[4,64,2,128]{3,1,0,2:T(8,128)} %get-tuple-element.144) | copy-start | bytes 786436
where the time goes:
time: 238 us; the launch traced here: 235 us
  blocking collectives  120 us (50%)
  matrix products  32.7 us (14%)
  local copies, waits for them, and re-layouts  32.1 us (13%)
  other arithmetic  27.5 us (12%)
  waiting for transfers between devices  11.3 us (5%)
  starting transfers between devices  10.3 us (4%)
    all_gather x6, blocking collectives, gathered_once(): both, at, found = (lax.all_gather(jnp.concatenate(lines), axis), 0, {})  86.3 us
    all_gather x1, blocking collectives, local(): lax.all_gather(normed, 'head', axis=1, tiled=True)  33.7 us
    dot_general x8, matrix products, block_advance(): jnp.einsum('hts,shj->thj', scores.astype(jnp.bfloat16), value_block, pref...  13.2 us
    dot_general x16, matrix products, state_increment(): jnp.einsum('shi,shj->hij', key_to_end, value_block, preferred_element_typ...  12.3 us
    all_to_all x1, waiting for transfers between devices, from_everyone(): return lax.all_to_all(copies, axis, split_axis=0, concat_axis=0, tiled=True)  11.3 us
    all_to_all x1, starting transfers between devices, from_everyone(): return lax.all_to_all(copies, axis, split_axis=0, concat_axis=0, tiled=True)  10.3 us
    exp x31, local copies, waits for them, and re-layouts, combine_states(): jnp.exp(latter[0])[:, None] * earlier[1] + latter[1]  9.35 us
    convert_element_type x8, other arithmetic, block_advance(): (key_block.astype(jnp.float32) * jnp.exp(-running)).astype(jnp.bfloat16)  7.31 us
  transfers between devices with their start and end apart: 1, of which 1 were waited for; matrix products, arithmetic and copies ran while one was open for 1% of the time, Pallas kernels for 0%

commit v1 on v0

--- a/solution.py
+++ b/solution.py
@@ -8,6 +8,13 @@
 HEAD_V = 128
 GROUP = 64
 SEQ = ("seq_0", "seq_1", "seq_2")
+
+
+def all_by_exchange(x, axis, d):
+    size = lax.axis_size(axis)
+    blocks = jnp.stack([x for _ in range(size)])
+    blocks = lax.all_to_all(blocks, axis, split_axis=0, concat_axis=0)
+    return jnp.concatenate(blocks, axis=d)
 
 
 def from_everyone(shard, axis):
@@ -194,9 +201,7 @@
     out_width = w_out.shape[1] // lax.axis_size("head")
     own_columns = lax.dynamic_slice_in_dim(w_out, lax.axis_index("head") * out_width, out_width, 1)
     encoded = jnp.dot(
-        lax.all_gather(normed, "head", axis=1, tiled=True),
-        own_columns,
-        preferred_element_type=jnp.float32,
+        all_by_exchange(normed, "head", 1), own_columns, preferred_element_type=jnp.float32
     )
     return encoded.astype(jnp.bfloat16)
 

time: 238 us -> 248 us (1.042)
  the two profiles are of different devices: /device:TPU:1 before, /device:TPU:8 now
where the time goes in v1:
time: 248 us; the launch traced here: 244 us
  blocking collectives  107 us (43%)
  waiting for transfers between devices  33.9 us (14%)
  local copies, waits for them, and re-layouts  32.8 us (13%)
  matrix products  32.7 us (13%)
  other arithmetic  27.3 us (11%)
  starting transfers between devices  9.66 us (4%)
    all_gather x6, blocking collectives, gathered_once(): both, at, found = (lax.all_gather(jnp.concatenate(lines), axis), 0, {})  107 us
    all_to_all x1, waiting for transfers between devices, all_by_exchange(): blocks = lax.all_to_all(blocks, axis, split_axis=0, concat_axis=0)  18.3 us
    all_to_all x1, waiting for transfers between devices, from_everyone(): return lax.all_to_all(copies, axis, split_axis=0, concat_axis=0, tiled=True)  15.6 us
    dot_general x8, matrix products, block_advance(): jnp.einsum('hts,shj->thj', scores.astype(jnp.bfloat16), value_block, pref...  13.2 us
    dot_general x16, matrix products, state_increment(): jnp.einsum('shi,shj->hij', key_to_end, value_block, preferred_element_typ...  12.3 us
    exp x31, local copies, waits for them, and re-layouts, combine_states(): jnp.exp(latter[0])[:, None] * earlier[1] + latter[1]  9.23 us
    convert_element_type x8, other arithmetic, block_advance(): (key_block.astype(jnp.float32) * jnp.exp(-running)).astype(jnp.bfloat16)  7.31 us
    unnamed x30, local copies, waits for them, and re-layouts  6.88 us
  transfers between devices with their start and end apart: 2, of which 2 were waited for; matrix products, arithmetic and copies ran while one was open for 1% of the time, Pallas kernels for 0%

profile of v1, /device:TPU:8, one launch (start us, length us, event | category | flops | bytes accessed | tf_op | source)
XLA Modules:
  0.0 244.3 jit_solution(8620672456260527433)
XLA Ops:
  2.0 6.2 %all-to-all-start = ((bf16[4,256,256]{1,2,0:T(8,128)(2,1)}), bf16[4,256,256]{1,2,0:T(8,128)(2,1)S(1)}, u32[]{:S(2)}, u32[]{:S(2)}) async-start(bf16[4,256,256]{1,2,0:T(8,128)(2,1)} %broadcast_in_dim.16), calls=%async_computation | async-start | bytes 1048576 | tf_op jit(solution)/shard_map/all_to_all | solution.py:22
  10.9 15.6 %all-to-all-done = bf16[4,256,256]{1,2,0:T(8,128)(2,1)S(1)} async-done(((bf16[4,256,256]{1,2,0:T(8,128)(2,1)}), bf16[4,256,256]{1,2,0:T(8,128)(2,1)S(1)}, u32[]{:S(2)}, u32[]{:S(2)}) %all-to-all-start) | async-done | bytes 524320 | tf_op jit(solution)/shard_map/all_to_all | solution.py:22
  31.6 2.8 %rev.21 = bf16[256,2,128]{2,0,1:T(8,128)(2,1)} reverse(bf16[256,2,128]{2,0,1:T(8,128)(2,1)} %copy.70), dimensions={0} | reverse | bytes 262144 | tf_op jit(solution)/shard_map/jit(_flip)/rev | solution.py:175
  36.2 4.5 %while.51 = (s32[]{:T(128)}, f32[2,64,128]{2,1,0:T(8,128)S(1)}, f32[4,64,2,64]{3,2,1,0:T(2,128)S(1)}, bf16[4,64,2,64]{3,2,1,0:T(2,128)(2,1)}, bf16[4,64,2,128]{3,1,2,0:T(8,128)(2,1)S(1)}, /*index=5*/s32[]{:T(128)}, s32[]{:T(128)}) while((s32[]{:T(128)}, f32[2,64,128]{2,1,0:T(8,128)S(1)}, f32[4,64,2,64]{3,2,1,0:T(2,128)S(1)}, ...), condition=%wide.region_9.10_spmd.clone, body=%wide.region_7.9_spmd.clone.sunk | while | flops 2695171 | bytes 364131 | solution.py:146
  40.8 11.9 %all-gather.9 = bf16[4,129,128]{2,1,0:T(8,128)(2,1)S(1)} all-gather(bf16[1,129,128]{2,1,0:T(8,128)(2,1)S(1)} %maximum_bitcast_fusion.3), channel_id=5, replica_groups=mesh['seq_0'=4,'seq_1'=8,'seq_2'=4,'head'=4] {'seq_2'}, dimensions={0}, use_global_device_ids=true | all-gather | bytes 165120 | tf_op jit(solution)/shard_map/all_gather | solution.py:50
  54.1 31.2 %all-gather.10 = bf16[8,129,128]{2,1,0:T(8,128)(2,1)S(1)} all-gather(bf16[1,129,128]{2,1,0:T(8,128)(2,1)S(1)} %maximum_bitcast_fusion.4), channel_id=6, replica_groups=mesh['seq_0'=4,'seq_1'=8,'seq_2'=4,'head'=4] {'seq_1'}, dimensions={0}, use_global_device_ids=true | all-gather | bytes 297216 | tf_op jit(solution)/shard_map/all_gather | solution.py:50
  86.5 1.7 copy.63
  88.3 1.7 copy.62
  90.0 7.6 %while.50 = (s32[]{:T(128)}, f32[2,64,128]{2,1,0:T(8,128)S(1)}, f32[4,64,2,64]{3,2,1,0:T(2,128)S(1)}, bf16[4,64,2,64]{3,2,1,0:T(2,128)(2,1)}, bf16[4,64,2,128]{3,1,2,0:T(8,128)(2,1)}, /*index=5*/s32[]{:T(128)}, s32[]{:T(128)}) while((s32[]{:T(128)}, f32[2,64,128]{2,1,0:T(8,128)S(1)}, f32[4,64,2,64]{3,2,1,0:T(2,128)S(1)}, ...), condition=%wide.region_2.3_spmd.clone, body=%wide.region_0.2_spmd.clone.sunk | while | flops 2695171 | bytes 347743 | solution.py:146
  97.6 13.9 %all-gather.6 = f32[4,129,128]{2,1,0:T(8,128)S(1)} all-gather(f32[1,129,128]{2,1,0:T(8,128)S(1)} %maximum_bitcast_fusion), channel_id=2, replica_groups=mesh['seq_0'=4,'seq_1'=8,'seq_2'=4,'head'=4] {'seq_2'}, dimensions={0}, use_global_device_ids=true | all-gather | bytes 330240 | tf_op jit(solution)/shard_map/all_gather | solution.py:50
  112.2 1.7 slice_convert_fusion.7
  114.1 25.3 %all-gather.7 = f32[8,129,128]{2,1,0:T(8,128)S(1)} all-gather(f32[1,129,128]{2,1,0:T(8,128)S(1)} %maximum_bitcast_fusion.1), channel_id=3, replica_groups=mesh['seq_0'=4,'seq_1'=8,'seq_2'=4,'head'=4] {'seq_1'}, dimensions={0}, use_global_device_ids=true | all-gather | bytes 594432 | tf_op jit(solution)/shard_map/all_gather | solution.py:50
  140.5 12.6 %all-gather.8 = f32[4,129,128]{2,1,0:T(8,128)S(1)} all-gather(f32[1,129,128]{2,1,0:T(8,128)S(1)} %maximum_bitcast_fusion.2), channel_id=4, replica_groups=mesh['seq_0'=4,'seq_1'=8,'seq_2'=4,'head'=4] {'seq_0'}, dimensions={0}, use_global_device_ids=true | all-gather | bytes 330240 | tf_op jit(solution)/shard_map/all_gather | solution.py:50
  154.0 12.0 %all-gather.11 = bf16[4,129,128]{2,1,0:T(8,128)(2,1)S(1)} all-gather(bf16[1,129,128]{2,1,0:T(8,128)(2,1)S(1)} %maximum_bitcast_fusion.5), channel_id=7, replica_groups=mesh['seq_0'=4,'seq_1'=8,'seq_2'=4,'head'=4] {'seq_0'}, dimensions={0}, use_global_device_ids=true | all-gather | bytes 165120 | tf_op jit(solution)/shard_map/all_gather | solution.py:50
  174.0 15.1 %while.48 = (s32[]{:T(128)}, f32[2,64,128]{2,1,0:T(8,128)S(1)}, f32[4,64,2,128]{3,1,0,2:T(8,128)}, f32[4,64,2,64]{3,2,1,0:T(2,128)S(1)}, bf16[4,64,2,64]{3,2,1,0...) while((s32[]{:T(128)}, f32[2,64,128]{2,1,0:T(8,128)S(1)}, ...), condition=%wide.region_6.7_spmd.clone, body=%wide.region_4.6_spmd.clone.sunk | while | flops 8011778 | bytes 774749 | solution.py:133
  175.1 1.6 fusion.262
  178.9 1.6 fusion.262
  182.7 1.6 fusion.262
  186.5 1.6 fusion.262
  202.0 15.1 %while.49 = (s32[]{:T(128)}, f32[2,64,128]{2,1,0:T(8,128)S(1)}, f32[4,64,2,128]{3,1,0,2:T(8,128)}, f32[4,64,2,64]{3,2,1,0:T(2,128)S(1)}, bf16[4,64,2,64]{3,2,1,0...) while((s32[]{:T(128)}, f32[2,64,128]{2,1,0:T(8,128)S(1)}, ...), condition=%wide.region_13.14_spmd.clone, body=%wide.region_11.13_spmd.clone.sunk | while | flops 8011778 | bytes 774749 | solution.py:133
  214.4 1.6 fusion.275
  217.1 1.7 rev.23
  221.5 3.5 %all-to-all-start.1 = ((bf16[4,256,256]{1,2,0:T(8,128)(2,1)}), bf16[4,256,256]{1,2,0:T(8,128)(2,1)S(1)}, u32[]{:S(2)}, u32[]{:S(2)}) async-start(bf16[4,256,256]{1,2,0:T(8,128)(2,1)} %stack.2), calls=%async_computation.1 | async-start | bytes 1048576 | tf_op jit(solution)/shard_map/all_to_all | solution.py:16
  224.9 18.3 %all-to-all-done.1 = bf16[4,256,256]{1,2,0:T(8,128)(2,1)S(1)} async-done(((bf16[4,256,256]{1,2,0:T(8,128)(2,1)}), bf16[4,256,256]{1,2,0:T(8,128)(2,1)S(1)}, u32[]{:S(2)}, u32[]{:S(2)}) %all-to-all-start.1) | async-done | bytes 524320 | tf_op jit(solution)/shard_map/all_to_all | solution.py:16
  (221 shorter events, 75.0 us)
Async XLA Ops:
  0.0 243.2 %copy-start = (bf16[1024,1024]{1,0:T(8,128)(2,1)S(1)}, bf16[1024,1024]{1,0:T(8,128)(2,1)}, u32[]{:S(2)}) copy-start(bf16[1024,1024]{1,0:T(8,128)(2,1)} %param.20) | copy-start | bytes 6291460
  0.0 8.2 %copy-start.5 = (bf16[2,256,128]{2,1,0:T(8,128)(2,1)S(1)}, bf16[2,256,128]{2,1,0:T(8,128)(2,1)}, u32[]{:S(2)}) copy-start(bf16[2,256,128]{2,1,0:T(8,128)(2,1)} %param.21) | copy-start | bytes 393220
  2.0 24.5 %all-to-all-start = ((bf16[4,256,256]{1,2,0:T(8,128)(2,1)}), bf16[4,256,256]{1,2,0:T(8,128)(2,1)S(1)}, u32[]{:S(2)}, u32[]{:S(2)}) async-start(bf16[4,256,256]{1,2,0:T(8,128)(2,1)} %broadcast_in_dim.16), calls=%async_computation | async-start | bytes 1048576 | tf_op jit(solution)/shard_map/all_to_all | solution.py:22
  40.8 56.8 %copy-start.1 = (bf16[4,64,2,128]{3,1,2,0:T(8,128)(2,1)}, bf16[4,64,2,128]{3,1,2,0:T(8,128)(2,1)S(1)}, u32[]{:S(2)}) copy-start(bf16[4,64,2,128]{3,1,2,0:T(8,128)(2,1)S(1)} %get-tuple-element.688) | copy-start | bytes 393220
  85.3 0.7 copy-start.2
  113.9 39.9 %copy-start.3 = (bf16[8,129,128]{2,1,0:T(8,128)(2,1)S(1)}, bf16[8,129,128]{2,1,0:T(8,128)(2,1)}, u32[]{:S(2)}) copy-start(bf16[8,129,128]{2,1,0:T(8,128)(2,1)} %copy-done.2) | copy-start | bytes 792580
  113.9 40.1 %copy-start.6 = (bf16[1,128]{1,0:T(2,128)(2,1)S(1)}, bf16[1,128]{1,0:T(2,128)(2,1)}, u32[]{:S(2)}) copy-start(bf16[1,128]{1,0:T(2,128)(2,1)} %convert_bitcast_fusion) | copy-start | bytes 772
  174.0 17.9 %copy-start.7 = (f32[1,1,128]{2,1,0:T(1,128)S(1)}, f32[1,1,128]{2,1,0:T(1,128)}, u32[]{:S(2)}) copy-start(f32[1,1,128]{2,1,0:T(1,128)} %get-tuple-element.415) | copy-start | bytes 1540
  174.0 24.5 %copy-start.10 = (f32[128]{0:T(128)S(1)}, f32[128]{0:T(128)}, u32[]{:S(2)}) copy-start(f32[128]{0:T(128)} %get-tuple-element.307) | copy-start | bytes 1540
  174.0 24.6 %copy-start.9 = (f32[128]{0:T(128)S(1)}, f32[128]{0:T(128)}, u32[]{:S(2)}) copy-start(f32[128]{0:T(128)} %get-tuple-element.308) | copy-start | bytes 1540
  174.0 24.7 %copy-start.8 = (f32[128]{0:T(128)S(1)}, f32[128]{0:T(128)}, u32[]{:S(2)}) copy-start(f32[128]{0:T(128)} %get-tuple-element.306) | copy-start | bytes 1540
  202.0 16.8 %copy-start.4 = (f32[4,64,2,128]{3,1,0,2:T(8,128)S(1)}, f32[4,64,2,128]{3,1,0,2:T(8,128)}, u32[]{:S(2)}) copy-start(f32[4,64,2,128]{3,1,0,2:T(8,128)} %get-tuple-element.144) | copy-start | bytes 786436
  221.5 21.8 %all-to-all-start.1 = ((bf16[4,256,256]{1,2,0:T(8,128)(2,1)}), bf16[4,256,256]{1,2,0:T(8,128)(2,1)S(1)}, u32[]{:S(2)}, u32[]{:S(2)}) async-start(bf16[4,256,256]{1,2,0:T(8,128)(2,1)} %stack.2), calls=%async_computation.1 | async-start | bytes 1048576 | tf_op jit(solution)/shard_map/all_to_all | solution.py:16
